TPU v7x, 32 devices: a whole 2x2x4 slice. The times are simulated.
32 devices in a mesh: ka: 4 (over y, x), ga: 8 (over z, core).
Axes of the slice: x: 2, y: 2, z: 4, core: 2. Of those that a mesh axis runs over, the one named last changes fastest.
Arguments:
- orbitals: bfloat16 [8, 8, 2, 32, 1024], P('ka', None, None, 'ga'), may hold values from -6 to 6
- band_counts: int32 [8], replicated, may hold values from 1 to 8, as said below
- pair_slot: int32 [8, 8], replicated, may hold values from 0 to 7
- kernel: float32 [8, 32, 1024], P(None, None, 'ga'), may hold values from 0.2 to 8
Outputs:
- exchange_vectors: float32 [8, 8, 2, 32, 1024], P('ka', None, None, 'ga')
- exchange_matrix: float32 [8, 2, 8, 8], P('ka')
- exchange_energy: float32 [], replicated
Inputs may be any that keep to these rules, and one draw needn't show every extreme that they name: The first band_counts[k] band slots of k-point k are the occupied ones; some k-point has all 8 slots occupied.
All inputs are finite; a program needn't handle non-finite values.
Results may differ from a plain program's by a relative error of at most 0.0003.
Values may be sent and summed in bfloat16 or wider, within the bound.
A program may use at most 128 MiB of HBM per device.

v0:
```python
import jax
import jax.numpy as jnp
from jax import lax
from jax.sharding import PartitionSpec as P

STEPS = 2


group_width = 2
highest = lax.Precision.HIGHEST


def passed_along(value, axis, steps):
    count = lax.axis_size(axis)
    pairs = [(source, (source + steps) % count) for source in range(count)]
    return lax.ppermute(value, axis, pairs)


def tables(points):
    positions = jnp.arange(points, dtype=jnp.int32)
    product = positions[:, None] * positions[None, :] % points
    angles = product.astype(jnp.float32) * (2.0 * jnp.pi / points)
    return (jnp.cos(angles), jnp.sin(angles))


def apply_table(table, values, dimension):
    rotated = jnp.tensordot(table, values, axes=([1], [dimension]), precision=highest)
    return jnp.moveaxis(rotated, 0, dimension)


def transform(real_part, imag_part, cosine_values, sine_values, dimension, forward):
    shifted = -sine_values if forward else sine_values
    first = apply_table(cosine_values, real_part + imag_part, dimension)
    second = apply_table(shifted - cosine_values, real_part, dimension)
    third = apply_table(cosine_values + shifted, imag_part, dimension)
    return (first - third, first + second)


def select_kernel(slot_ids, kernel_flat):
    slot_total = kernel_flat.shape[0]
    onehot = (slot_ids[:, None] == jnp.arange(slot_total, dtype=jnp.int32)[None, :]).astype(
        jnp.float32
    )
    return jnp.dot(onehot, kernel_flat, precision=highest, preferred_element_type=jnp.float32)


def contract(first_field, second_field):
    return jnp.einsum("kar,kbr->kab", first_field, second_field, precision=highest)


def on_device(orbitals, band_counts, pair_slot, kernel):
    local_kpoints = orbitals.shape[0]
    band_count = orbitals.shape[1]
    planes = orbitals.shape[3]
    columns = orbitals.shape[4]
    points = kernel.shape[1]
    groups = lax.axis_size("ka")
    kpoints = local_kpoints * groups
    own_group = lax.axis_index("ka")
    cosine_values, sine_values = tables(points)
    volume = float(points * points * points)
    weight = -1.0 / kpoints
    band_index = jnp.arange(band_count, dtype=jnp.int32)
    own_counts = lax.dynamic_slice_in_dim(band_counts, own_group * local_kpoints, local_kpoints)

    def masked(block_data, counts):
        keep = (band_index[None, :] < counts[:, None]).astype(orbitals.dtype)
        return block_data * keep[:, :, None, None, None]

    def slot_table(anchor):
        own_rows = lax.dynamic_slice_in_dim(pair_slot, own_group * local_kpoints, local_kpoints, 0)
        return lax.dynamic_slice_in_dim(own_rows, anchor * local_kpoints, local_kpoints, 1)

    row_count = local_kpoints * band_count * local_kpoints // lax.axis_size("ga")
    gathered_own = lax.all_gather(orbitals, "ga", axis=3, tiled=True)
    gathered_kernel = lax.all_gather(kernel, "ga", axis=2, tiled=True)
    kernel_flat = gathered_kernel.reshape(gathered_kernel.shape[0], -1)
    row_ids = lax.axis_index("ga") * row_count + jnp.arange(row_count, dtype=jnp.int32)
    own_row = row_ids // local_kpoints
    peer_row = row_ids % local_kpoints
    own_kpoint = own_row // band_count
    own_field = jnp.take(
        gathered_own.reshape(local_kpoints * band_count, 2, points, columns), own_row, axis=0
    )
    own_field = jnp.transpose(own_field.astype(jnp.float32), (1, 2, 3, 0))
    kpoint_index = jnp.arange(local_kpoints, dtype=jnp.int32)
    totals = (
        jnp.zeros((points, columns, row_count), jnp.float32),
        jnp.zeros((points, columns, row_count), jnp.float32),
    )

    def handle(current, anchor, totals):
        counts = lax.dynamic_slice_in_dim(band_counts, anchor * local_kpoints, local_kpoints)
        gathered = lax.all_gather(masked(current, counts), "ga", axis=3, tiled=True)
        incoming = jnp.transpose(
            jnp.take(gathered, peer_row, axis=0).astype(jnp.float32), (2, 3, 4, 0, 1)
        )
        slot_grid = slot_table(anchor)
        matches = (own_kpoint[:, None, None] == kpoint_index[None, :, None]) & (
            peer_row[:, None, None] == kpoint_index[None, None, :]
        )
        slot_ids = jnp.sum(jnp.where(matches, slot_grid[None], 0), axis=(1, 2))
        chosen = select_kernel(slot_ids, kernel_flat).reshape(row_count, points, points, points)
        chosen = jnp.transpose(chosen, (1, 2, 3, 0))[..., None]
        row_counts = jnp.sum(
            jnp.where(peer_row[:, None] == kpoint_index[None, :], counts[None, :], 0), axis=1
        )
        trip_count = (jnp.max(row_counts) + group_width - 1) // group_width

        def one_group(group_turn, totals):
            picked = lax.dynamic_slice_in_dim(incoming, group_turn * group_width, group_width, 4)
            real_part = own_field[0][..., None] * picked[0] + own_field[1][..., None] * picked[1]
            imag_part = own_field[1][..., None] * picked[0] - own_field[0][..., None] * picked[1]
            real_part = real_part.reshape(points, points, points, row_count * group_width)
            imag_part = imag_part.reshape(points, points, points, row_count * group_width)
            real_part, imag_part = transform(
                real_part, imag_part, cosine_values, sine_values, 2, True
            )
            real_part, imag_part = transform(
                real_part, imag_part, cosine_values, sine_values, 1, True
            )
            real_part, imag_part = transform(
                real_part, imag_part, cosine_values, sine_values, 0, True
            )
            real_part = (
                real_part.reshape(points, points, points, row_count, group_width) * chosen
            ).reshape(points, points, points, row_count * group_width)
            imag_part = (
                imag_part.reshape(points, points, points, row_count, group_width) * chosen
            ).reshape(points, points, points, row_count * group_width)
            real_part, imag_part = transform(
                real_part, imag_part, cosine_values, sine_values, 0, False
            )
            real_part, imag_part = transform(
                real_part, imag_part, cosine_values, sine_values, 1, False
            )
            real_part, imag_part = transform(
                real_part, imag_part, cosine_values, sine_values, 2, False
            )
            real_part = real_part.reshape(points, columns, row_count, group_width) / volume
            imag_part = imag_part.reshape(points, columns, row_count, group_width) / volume
            add_real = jnp.sum(picked[0] * real_part - picked[1] * imag_part, axis=3)
            add_imag = jnp.sum(picked[0] * imag_part + picked[1] * real_part, axis=3)
            return (totals[0] + weight * add_real, totals[1] + weight * add_imag)

        return lax.fori_loop(0, trip_count, one_group, totals)

    block_data = orbitals
    for rotation in range(STEPS):
        anchor = (own_group - rotation) % groups
        current = block_data
        totals = handle(current, anchor, totals)
        if rotation + 1 < STEPS:
            block_data = passed_along(block_data, "ka", 1)
    row_fields = jnp.transpose(jnp.stack(totals), (3, 0, 1, 2))
    spread = lax.all_to_all(row_fields, "ga", split_axis=2, concat_axis=0, tiled=True)
    vectors = jnp.sum(
        spread.reshape(local_kpoints, band_count, local_kpoints, 2, planes, columns), axis=2
    )
    flat_orbitals = orbitals.astype(jnp.float32).reshape(
        local_kpoints, band_count, 2, planes * columns
    )
    flat_vectors = vectors.reshape(local_kpoints, band_count, 2, planes * columns)
    matrix_real = (
        contract(flat_orbitals[:, :, 0], flat_vectors[:, :, 0])
        + contract(flat_orbitals[:, :, 1], flat_vectors[:, :, 1])
    ) / volume
    matrix_imag = (
        contract(flat_orbitals[:, :, 0], flat_vectors[:, :, 1])
        - contract(flat_orbitals[:, :, 1], flat_vectors[:, :, 0])
    ) / volume
    matrix = lax.psum(jnp.stack((matrix_real, matrix_imag), axis=1), "ga")
    occupied = (band_index[None, :] < own_counts[:, None]).astype(jnp.float32)
    energy_part = jnp.sum(occupied * jnp.diagonal(matrix[:, 0], axis1=1, axis2=2)) / (2.0 * kpoints)
    energy = lax.psum(energy_part, "ka")
    return (vectors, matrix, energy)


def solution(mesh):
    in_specs = (P("ka", None, None, "ga", None), P(), P(), P(None, None, "ga"))
    out_specs = (P("ka", None, None, "ga", None), P("ka", None, None, None), P())
    return jax.shard_map(
        on_device, mesh=mesh, in_specs=in_specs, out_specs=out_specs, check_vma=False
    )
```

profile of v0, /device:TPU:0, one launch (start us, length us, event | category | flops | bytes accessed | tf_op | source)
XLA Modules:
  0.0 1977.2 jit_solution(4263347270041743615)
XLA Ops:
  27.4 8.8 all-gather.9.cloned.1.call-done
  71.5 25.0 %all-gather.5.cloned.1.call-done = bf16[2,8,2,32,1024]{4,1,2,0,3:T(8,128)(2,1)} async-done(((bf16[2,8,2,4,1024]{4,1,2,0,3:T(8,128)(2,1)}), bf16[2,8,2,32,1024]{4,1,2,0,3:T(8,128)(2,1)}) %all-gather.5.cloned.1.call-update) | async-done | bytes 2097168 | tf_op jit(solution)/shard_map/all_gather | solution.py:94
  102.0 24.5 %all-gather.11.cloned.1.call-done = bf16[2,8,2,32,1024]{4,1,2,0,3:T(8,128)(2,1)} async-done(((bf16[2,8,2,4,1024]{4,1,2,0,3:T(8,128)(2,1)}), bf16[2,8,2,32,1024]{4,1,2,0,3:T(8,128)(2,1)}) %all-gather.11.cloned.1.call-update) | async-done | bytes 2097168 | tf_op jit(solution)/shard_map/all_gather | solution.py:94
  132.1 10.3 convert_bitcast_fusion
  144.3 870.9 %while.32 = (s32[]{:T(128)}, f32[32,1024,4]{1,2,0:T(4,128)}, f32[32,1024,4]{1,2,0:T(4,128)}, s32[]{:T(128)}, f32[2,32,1024,4,8]{2,1,0,4,3:T(8,128)}, /*index=5*/...) while((s32[]{:T(128)}, f32[32,1024,4]{1,2,0:T(4,128)}, ...), condition=%wide.region_6.8_spmd.clone.clone, body=%wide.region_3.7_spmd.clone.clone.sunk | while | flops 1821915136 | bytes 157811248 | solution.py:146
  171.0 10.3 multiply_subtract_fusion.4
  211.2 9.1 fusion.470
  326.7 8.7 multiply_bitcast_fusion.9
  388.3 10.3 multiply_subtract_fusion.4
  428.4 9.1 fusion.470
  544.0 8.7 multiply_bitcast_fusion.9
  605.5 10.3 multiply_subtract_fusion.4
  645.7 9.1 fusion.470
  822.8 10.3 multiply_subtract_fusion.4
  862.9 9.1 fusion.470
  978.5 8.7 multiply_bitcast_fusion.9
  1015.2 879.5 %while.33 = (s32[]{:T(128)}, f32[32,1024,4]{1,2,0:T(4,128)}, f32[32,1024,4]{1,2,0:T(4,128)}, s32[]{:T(128)}, f32[2,32,1024,4,8]{2,1,0,4,3:T(8,128)}, /*index=5*/...) while((s32[]{:T(128)}, f32[32,1024,4]{1,2,0:T(4,128)}, ...), condition=%wide.region_13.15_spmd.clone.clone, body=%wide.region_10.14_spmd.clone.clone.sunk | while | flops 1821915136 | bytes 157811248 | solution.py:146
  1047.3 10.3 multiply_subtract_fusion.5
  1087.6 9.2 fusion.510
  1203.3 8.7 multiply_bitcast_fusion.11
  1264.9 10.3 multiply_subtract_fusion.5
  1305.1 9.2 fusion.510
  1420.8 8.7 multiply_bitcast_fusion.11
  1482.4 10.3 multiply_subtract_fusion.5
  1522.6 9.2 fusion.510
  1638.3 8.7 multiply_bitcast_fusion.11
  1699.9 10.3 multiply_subtract_fusion.5
  1740.1 9.2 fusion.510
  1855.8 8.7 multiply_bitcast_fusion.11
  1901.2 26.3 %all-to-all-done = f32[4,2,32,1024]{3,0,1,2:T(4,128)S(1)} async-done(((f32[4,2,32,1024]{3,0,1,2:T(4,128)}), f32[4,2,32,1024]{3,0,1,2:T(4,128)S(1)}, u32[]{:S(2)}, u32[]{:S(2)}) %all-to-all-start) | async-done | bytes 1048608 | tf_op jit(solution)/shard_map/all_to_all | solution.py:156
  1930.7 26.7 %psum.14 = f32[2,2,8,8]{3,2,0,1:T(8,128)S(1)} all-reduce(f32[2,2,8,8]{3,2,0,1:T(8,128)S(1)} %pad_maximum_fusion), channel_id=1, replica_groups=mesh['ka'=4,'ga'=8] {'ga'}, use_global_device_ids=true, to_apply=%region_15.17 | all-reduce | flops 256 | bytes 2048 | tf_op jit(solution)/shard_map/psum | solution.py:172
  1960.0 10.3 psum.15
  (560 shorter events, 1597.0 us)
Async XLA Ops:
  7.2 29.0 %all-gather.9.cloned.1.call-start = ((), (), s32[]{:S(2)}) async-start(), calls=%async_computation.3 | async-start | bytes 1179648 | tf_op jit(solution)/shard_map/all_gather | solution.py:76
  7.9 58.4 %all-gather.7.cloned.1.call-start = ((), (), s32[]{:S(2)}) async-start(), calls=%async_computation.2 | async-start | bytes 2359296 | tf_op jit(solution)/shard_map/all_gather | solution.py:75
  11.5 85.0 %all-gather.5.cloned.1.call-start = ((), (), s32[]{:S(2)}) async-start(), calls=%async_computation.1 | async-start | bytes 2359296 | tf_op jit(solution)/shard_map/all_gather | solution.py:94
  12.3 114.3 %all-gather.11.cloned.1.call-start = ((), (), s32[]{:S(2)}) async-start(), calls=%async_computation.4 | async-start | bytes 2359296 | tf_op jit(solution)/shard_map/all_gather | solution.py:94
  12.3 10.5 collective-permute-start
  290.5 8.8 copy-start.12
  311.5 8.1 copy-start
  348.7 11.2 copy-start.16
  507.8 8.8 copy-start.12
  528.7 8.1 copy-start
  566.0 11.2 copy-start.16
  725.0 8.8 copy-start.12
  746.0 8.1 copy-start
  783.2 11.2 copy-start.16
  942.3 8.8 copy-start.12
  963.2 8.1 copy-start
  1000.5 11.2 copy-start.16
  1167.2 8.7 copy-start.13
  1188.0 8.1 copy-start.1
  1225.3 11.2 copy-start.18
  1384.7 8.7 copy-start.13
  1405.5 8.1 copy-start.1
  1442.8 11.2 copy-start.18
  1602.2 8.7 copy-start.13
  1623.0 8.1 copy-start.1
  1660.3 11.2 copy-start.18
  1819.7 8.7 copy-start.13
  1840.5 8.1 copy-start.1
  1877.8 11.2 copy-start.18
  1897.3 60.8 %copy-start.26 = (s32[2]{0:T(128)S(1)}, s32[2]{0:T(128)}, u32[]{:S(2)}) copy-start(s32[2]{0:T(128)} %get-tuple-element.610) | copy-start | bytes 28
  1897.3 30.2 %all-to-all-start = ((f32[4,2,32,1024]{3,0,1,2:T(4,128)}), f32[4,2,32,1024]{3,0,1,2:T(4,128)S(1)}, u32[]{:S(2)}, u32[]{:S(2)}) async-start(f32[4,2,32,1024]{3,0,1,2:T(4,128)} %maximum_bitcast_fusion), calls=%async_computation | async-start | bytes 2097152 | tf_op jit(solution)/shard_map/all_to_all | solution.py:156
  1928.7 41.6 %copy-start.24 = (f32[2,8,2,4,1024]{4,3,2,1,0:T(4,128)}, f32[2,8,2,4,1024]{4,3,2,1,0:T(4,128)S(1)}, u32[]{:S(2)}) copy-start(f32[2,8,2,4,1024]{4,3,2,1,0:T(4,128)S(1)} %reduce_sum.102) | copy-start | bytes 1572868
  (73 other events, 245.0 us)
Sparse Core Ops, SparseCore 0:
  9.6 26.5 all-gather.8
  38.4 27.8 all-gather.6
  67.9 28.5 all-gather.4
  97.9 28.5 all-gather.10
where the time goes:
time: 1990 us; the launch traced here: 1980 us
  matrix products  912 us (46%)
  local copies, waits for them, and re-layouts  733 us (37%)
  other arithmetic  157 us (8%)
  waiting for transfers between devices  101 us (5%)
  blocking collectives  37 us (2%)
    dot_general x144, matrix products, apply_table(): jnp.tensordot(table, values, axes=([1], [dimension]), precision=highest)  897 us
    sub x16, local copies, waits for them, and re-layouts, transform(): return (first - third, first + second)  112 us
    add x16, local copies, waits for them, and re-layouts, transform(): first = apply_table(cosine_values, real_part + imag_part, dimension)  111 us
    add x16, local copies, waits for them, and re-layouts, transform(): return (first - third, first + second)  111 us
    while x208, local copies, waits for them, and re-layouts  87.8 us
    sub x8, other arithmetic, one_group(): own_field[1][..., None] * picked[0] - own_field[0][..., None] * picked[1]  82.5 us
    mul x24, local copies, waits for them, and re-layouts, one_group(): own_field[0][..., None] * picked[0] + own_field[1][..., None] * picked[1]  57.8 us
    reduce_sum x8, other arithmetic, one_group(): add_imag = jnp.sum(picked[0] * imag_part + picked[1] * real_part, axis=3)  50.1 us
  transfers between devices with their start and end apart: 6, of which 6 were waited for; matrix products, arithmetic and copies ran while one was open for 2% of the time, Pallas kernels for 0%

commit v1 on v0

v1 whole, which is shorter than its diff:
```python
import jax
import jax.numpy as jnp
import numpy as np
from jax import lax
from jax.experimental import pallas as pl
from jax.experimental.pallas import tpu as pltpu
from jax.sharding import PartitionSpec as P

STEPS = 2
LANES = 128


def split_np(matrix):
    high = matrix.astype(np.float32).astype(jnp.bfloat16)
    low = (matrix - high.astype(np.float64)).astype(np.float32).astype(jnp.bfloat16)
    return high, low


def real_form(matrix):
    return np.block([[matrix.real, -matrix.imag], [matrix.imag, matrix.real]])


def build_tables(points, members):
    wide = LANES // points
    quads = points // (2 * wide)
    planes = points // members
    dft = np.exp(-2j * np.pi * np.outer(np.arange(points), np.arange(points)) / points)
    x_of = np.arange(points).reshape(members, 1, planes)
    y1_of = np.arange(quads).reshape(1, quads, 1)
    x_of, y1_of = (np.broadcast_to(v, (members, quads, planes)).reshape(-1) for v in (x_of, y1_of))
    gx = np.tile(np.arange(points), quads)
    q = np.repeat(np.arange(quads), points)
    left, left_back = [], []
    for p in range(2):
        phase = np.outer(gx, x_of) / points + np.outer(p + 2 * q, y1_of) * wide / points
        forward = np.exp(-2j * np.pi * phase)
        high, low = split_np(real_form(forward))
        left.append(np.concatenate([high, low, high], axis=1))
        high, low = split_np(real_form(np.conj(forward).T))
        left_back.append(np.concatenate([high, low, high], axis=1))
    small = np.exp(-2j * np.pi * np.outer(np.arange(wide), np.arange(wide)) / wide)
    lane = np.kron(small, dft)
    right = []
    for matrix in (lane, np.conj(lane)):
        high, low = split_np(real_form(matrix).T)
        right.append(np.concatenate([high, low, high], axis=0))
    low_freq = (np.arange(2)[:, None] + 2 * np.arange(quads)[None, :]).reshape(-1)
    y0 = np.repeat(np.arange(wide), points)
    twiddle = np.exp(-2j * np.pi * np.outer(low_freq, y0) / points)
    twiddle = np.stack([twiddle.real, twiddle.imag]).astype(np.float32)
    return np.stack(left), np.stack(left_back), right[0], right[1], twiddle


def split(values):
    high = values.astype(jnp.bfloat16)
    low = (values - high.astype(jnp.float32)).astype(jnp.bfloat16)
    return high, low


def pair_kernel(rows, bands, windows, points, info, block, kernel, left, left_back, right, right_back,
                twiddle, out, projections, own, other, total):
    members = block.shape[0]
    piece = block.shape[3] // 2
    tall = members * piece
    quads = tall // points

    def load(orbital, part, h):
        value = block[:, orbital, part, h * piece:(h + 1) * piece, :]
        return value.astype(jnp.float32).reshape(tall, LANES)

    first_row = info[2 * windows]
    first_band = info[2 * windows + 1]
    for r in range(rows):
        for part in range(2):
            for h in range(2):
                own[r, part, h] = load(first_row + r, part, h)
    total[...] = jnp.zeros_like(total)

    def rotate(real_part, imag_part, p, sign):
        cos = twiddle[0, p * quads:(p + 1) * quads, :].reshape(quads, 1, LANES)
        sin = twiddle[1, p * quads:(p + 1) * quads, :].reshape(quads, 1, LANES) * sign
        real_part = real_part.reshape(quads, points, LANES)
        imag_part = imag_part.reshape(quads, points, LANES)
        new_real = real_part * cos - imag_part * sin
        new_imag = imag_part * cos + real_part * sin
        return new_real.reshape(tall, LANES), new_imag.reshape(tall, LANES)

    def dot(a, b):
        return jnp.dot(a, b, preferred_element_type=jnp.float32)

    def from_left(matrix, values):
        high, low = split(values)
        return dot(matrix, jnp.concatenate([high, high, low], axis=0))

    def from_right(values, matrix):
        high, low = split(values)
        return dot(jnp.concatenate([high, high, low], axis=1), matrix)

    def window_body(w, carry):
        slot = info[windows + w]

        def band_body(b, carry):
            orbital = w * bands + b
            for part in range(2):
                for h in range(2):
                    other[part, h] = load(orbital, part, h)
            inputs = ([], [])
            for r in range(rows):
                fields = []
                for h in range(2):
                    real_part = own[r, 0, h] * other[0, h] + own[r, 1, h] * other[1, h]
                    imag_part = own[r, 1, h] * other[0, h] - own[r, 0, h] * other[1, h]
                    fields.append(jnp.concatenate([real_part, imag_part], axis=0))
                inputs[0].append(fields[0] + fields[1])
                inputs[1].append(fields[0] - fields[1])
            turned = []
            for p in range(2):
                spectrum = from_left(left[p], jnp.concatenate(inputs[p], axis=1))
                for r in range(rows):
                    cut = spectrum[:, r * LANES:(r + 1) * LANES]
                    turned.append(jnp.concatenate(rotate(cut[:tall], cut[tall:], p, 1.0), axis=1))
            back = ([], [])
            for p in range(2):
                chosen = kernel[slot, p * tall:(p + 1) * tall, :]
                chosen = jnp.concatenate([chosen, chosen], axis=1)
                for r in range(rows):
                    full = from_right(turned[p * rows + r], right[...]) * chosen
                    full = from_right(full, right_back[...])
                    pair = rotate(full[:, :LANES], full[:, LANES:], p, -1.0)
                    back[p].append(jnp.concatenate(pair, axis=0))
            halves = [from_left(left_back[p], jnp.concatenate(back[p], axis=1)) for p in range(2)]
            for h in range(2):
                potential = halves[0] + halves[1] if h == 0 else halves[0] - halves[1]
                for r in range(rows):
                    real_part = potential[:tall, r * LANES:(r + 1) * LANES]
                    imag_part = potential[tall:, r * LANES:(r + 1) * LANES]
                    total[r, 0, h] += other[0, h] * real_part - other[1, h] * imag_part
                    total[r, 1, h] += other[0, h] * imag_part + other[1, h] * real_part
            return carry

        return lax.fori_loop(0, info[w], band_body, carry)

    lax.fori_loop(0, windows, window_body, 0)
    for r in range(rows):
        for part in range(2):
            for h in range(2):
                out[:, r, part, h * piece:(h + 1) * piece, :] = total[r, part, h].reshape(members, piece, LANES)

    def project(a, carry):
        for part in range(2):
            for h in range(2):
                other[part, h] = load(first_band + a, part, h)
        for r in range(rows):
            real_sum = jnp.zeros((tall, LANES), jnp.float32)
            imag_sum = jnp.zeros((tall, LANES), jnp.float32)
            for h in range(2):
                real_sum += other[0, h] * total[r, 0, h] + other[1, h] * total[r, 1, h]
                imag_sum += other[0, h] * total[r, 1, h] - other[1, h] * total[r, 0, h]
            projections[r, a] = jnp.concatenate(
                [jnp.sum(real_sum, axis=0, keepdims=True), jnp.sum(imag_sum, axis=0, keepdims=True)], axis=0)
        return carry

    lax.fori_loop(0, bands, project, 0)


def on_device(orbitals, band_counts, pair_slot, kernel):
    local, bands, _, planes, columns = orbitals.shape
    slots, points = kernel.shape[0], kernel.shape[1]
    members = lax.axis_size("ga")
    groups = lax.axis_size("ka")
    kpoints = local * groups
    group, member = lax.axis_index("ka"), lax.axis_index("ga")
    volume = float(points ** 3)
    wide = LANES // points
    quads = points // (2 * wide)
    tiles = columns // LANES
    rows = max(1, local * bands // members)
    share = max(1, members // (local * bands))
    windows = STEPS * local
    tables = build_tables(points, members)

    pieces = orbitals.reshape(local * bands, 2, planes, tiles, LANES).transpose(0, 1, 3, 2, 4)
    pieces = pieces.reshape(local * bands, 2, tiles * planes, LANES)
    blocks = [pieces]
    pairs = [(source, (source + 1) % groups) for source in range(groups)]
    for _ in range(STEPS - 1):
        blocks.append(lax.ppermute(blocks[-1], "ka", pairs))
    gathered = lax.all_gather(jnp.concatenate(blocks, axis=0), "ga", axis=0)

    whole = lax.all_gather(kernel, "ga", axis=2, tiled=True) * (-1.0 / (kpoints * volume))
    whole = whole.reshape(slots, points, wide, quads, 2, points).transpose(0, 4, 3, 1, 2, 5)
    whole = whole.reshape(slots, 2 * quads * points, LANES)

    first_row = member // share * rows
    own_kpoint = first_row // bands
    anchors = (group - jnp.arange(STEPS, dtype=jnp.int32)) % groups
    window = (anchors[:, None] * local + jnp.arange(local, dtype=jnp.int32)[None, :]).reshape(-1)
    slot_row = lax.dynamic_index_in_dim(pair_slot, group * local + own_kpoint, 0, keepdims=False)
    mine = jnp.arange(windows, dtype=jnp.int32) % share == member % share
    info = jnp.concatenate([jnp.where(mine, band_counts[window], 0), slot_row[window],
                            jnp.stack([first_row, own_kpoint * bands]).astype(jnp.int32)])

    tall = quads * points
    field = (rows, 2, 2, tall, LANES)
    smem = pl.BlockSpec(memory_space=pltpu.SMEM)
    vmem = pl.BlockSpec(memory_space=pltpu.VMEM)

    def body(*refs):
        pair_kernel(rows, bands, windows, points, *refs)

    spread, projections = pl.pallas_call(
        body,
        out_shape=(jax.ShapeDtypeStruct((members, rows, 2, tiles * planes, LANES), jnp.float32),
                   jax.ShapeDtypeStruct((rows, bands, 2, LANES), jnp.float32)),
        in_specs=[smem] + [vmem] * 7,
        out_specs=(vmem, vmem),
        scratch_shapes=[pltpu.VMEM(field, jnp.float32), pltpu.VMEM(field[1:], jnp.float32),
                        pltpu.VMEM(field, jnp.float32)],
        compiler_params=pltpu.CompilerParams(vmem_limit_bytes=48 * 2 ** 20),
        name="pairs",
    )(info, gathered, whole, *[jnp.asarray(table) for table in tables])

    vectors = lax.all_to_all(spread, "ga", split_axis=0, concat_axis=0, tiled=True)
    if share > 1:
        vectors = jnp.sum(vectors.reshape(local * bands, share, *vectors.shape[1:]), axis=1)
    vectors = vectors.reshape(local, bands, 2, tiles, planes, LANES).transpose(0, 1, 2, 4, 3, 5)
    vectors = vectors.reshape(local, bands, 2, planes, columns)
    sums = jnp.sum(projections, axis=-1) / volume
    sums = lax.all_gather(sums, ("ka", "ga"), axis=0)
    sums = jnp.sum(sums.reshape(kpoints, bands, share, bands, 2), axis=2)
    everything = sums.transpose(0, 3, 2, 1)
    matrix = lax.dynamic_slice_in_dim(everything, group * local, local, 0)
    occupied = (jnp.arange(bands)[None, :] < band_counts[:, None]).astype(jnp.float32)
    energy = jnp.sum(occupied * jnp.diagonal(everything[:, 0], axis1=1, axis2=2)) / (2.0 * kpoints)
    return (vectors, matrix, energy)


def solution(mesh):
    in_specs = (P("ka", None, None, "ga", None), P(), P(), P(None, None, "ga"))
    out_specs = (P("ka", None, None, "ga", None), P("ka", None, None, None), P())
    return jax.shard_map(
        on_device, mesh=mesh, in_specs=in_specs, out_specs=out_specs, check_vma=False
    )
```

time: 1990 us -> 183 us (0.09)
  matrix products: 912 us -> 0 us
  local copies, waits for them, and re-layouts: 733 us -> 18.7 us
  other arithmetic: 157 us -> 3.97 us
  waiting for transfers between devices: 101 us -> 54 us
  Pallas kernels: 0 us -> 40.2 us
    dot_general x150 -> x0, matrix products: 912 us -> none  [the longest x144 897 us: apply_table(): jnp.tensordot(table, values, axes=([1], [dimension]), precision=highest)]
    add x32 -> x1, local copies, waits for them, and re-layouts: 221 us -> 0.08 us  [on_device(): anchors[:, None] * local + jnp.arange(local, dtype=jnp.int32)[None, :]]
    mul x48 -> x0, local copies, waits for them, and re-layouts: 121 us -> none  [the longest x24 57.8 us: one_group(): own_field[0][..., None] * picked[0] + own_field[1][..., None] * picked[1]]
    sub x16 -> x0, local copies, waits for them, and re-layouts: 112 us -> none  [transform(): return (first - third, first + second)]
    while x208 -> x0, local copies, waits for them, and re-layouts: 87.8 us -> none
    sub x8 -> x0, other arithmetic: 82.5 us -> none  [one_group(): own_field[1][..., None] * picked[0] - own_field[0][..., None] * picked[1]]
    div x18 -> x1, local copies, waits for them, and re-layouts: 77.7 us -> 0.09 us  [on_device(): sums = jnp.sum(projections, axis=-1) / volume]
    squeeze x18 -> x2, local copies, waits for them, and re-layouts: 67.1 us -> 0.01 us  [the longest x1 0.01 us: on_device(): lax.dynamic_index_in_dim(pair_slot, group * local + own_kpoint, 0, keepdi...]
  transfers between devices with their start and end apart: 6 -> 4, of which waited for: 6 -> 3; matrix products, arithmetic and copies ran while one was open for 2% -> 12% of each run, Pallas kernels for 0% -> 0%
where the time goes in v1:
time: 183 us; the launch traced here: 184 us
  waiting for transfers between devices  54 us (30%)
  blocking collectives  44.4 us (24%)
  Pallas kernels  40.2 us (22%)
  local copies, waits for them, and re-layouts  18.7 us (10%)
  between operations  16 us (9%)
  starting transfers between devices  6.59 us (4%)
  other arithmetic  3.97 us (2%)
    all_gather x1, blocking collectives, on_device(): sums = lax.all_gather(sums, ('ka', 'ga'), axis=0)  44.4 us
    pallas_call x1, Pallas kernels, on_device(): pl.pallas_call(body, out_shape=(jax.ShapeDtypeStruct((members, rows, 2, t...  40.2 us
    all_gather x1, waiting for transfers between devices, on_device(): gathered = lax.all_gather(jnp.concatenate(blocks, axis=0), 'ga', axis=0)  32.1 us
    all_gather x1, waiting for transfers between devices, on_device(): lax.all_gather(kernel, 'ga', axis=2, tiled=True)  13.7 us
    reshape x2, local copies, waits for them, and re-layouts, on_device(): whole.reshape(slots, points, wide, quads, 2, points)  10.5 us
    ppermute x1, waiting for transfers between devices, on_device(): blocks.append(lax.ppermute(blocks[-1], 'ka', pairs))  7.47 us
    reshape x1, local copies, waits for them, and re-layouts, on_device(): whole = whole.reshape(slots, 2 * quads * points, LANES)  3.9 us
  transfers between devices with their start and end apart: 4, of which 3 were waited for; matrix products, arithmetic and copies ran while one was open for 12% of the time, Pallas kernels for 0%

profile of v1, /device:TPU:0, one launch (start us, length us, event | category | flops | bytes accessed | tf_op | source)
XLA Modules:
  0.0 183.8 jit_solution(63569584519819367)
XLA Ops:
  7.2 0.0 copy-start
  7.2 0.0 all-gather.5.cloned.1.call-start
  7.2 0.7 all-gather.5.cloned.1.call-update
  7.9 0.0 all-gather.7.cloned.1.call-start
  8.0 3.0 %collective-permute-start = (bf16[16,2,32,128]{3,2,1,0:T(8,128)(2,1)}, bf16[16,2,32,128]{3,2,1,0:T(8,128)(2,1)S(1)}, u32[]{:S(2)}, u32[]{:S(2)}) collective-permute-start(bf16[16,2,32,128]{3,2,1,0:T(8,128)(2,1)} %bitcast.38), channel_id=1, source_target_pairs={{0,8},{8,16},{16,24},{24,0},{1,9},{9,17},{17,25},{25,1},{2,10},{10... | collective-permute-start | bytes 786440 | tf_op jit(solution)/shard_map/ppermute | solution.py:187
  11.0 7.5 %collective-permute-done = bf16[16,2,32,128]{3,2,1,0:T(8,128)(2,1)S(1)} collective-permute-done((bf16[16,2,32,128]{3,2,1,0:T(8,128)(2,1)}, bf16[16,2,32,128]{3,2,1,0:T(8,128)(2,1)S(1)}, u32[]{:S(2)}, u32[]{:S(2)}) %collective-permute-start) | collective-permute-done | bytes 262176 | tf_op jit(solution)/shard_map/ppermute | solution.py:187
  18.5 1.8 pad_maximum_fusion
  20.2 0.0 all-gather.7.cloned.1.call-update
  20.3 0.1 iota_add_fusion
  20.4 0.1 add.71
  20.5 0.6 gather_fusion.1
  21.1 1.3 gather_fusion
  22.4 0.1 pad_add_fusion.refs_0_
  22.5 13.7 %all-gather.5.cloned.1.call-done = f32[8,32,1024]{2,1,0:T(8,128)} async-done(((f32[8,32,128]{2,1,0:T(8,128)}), f32[8,32,1024]{2,1,0:T(8,128)}) %all-gather.5.cloned.1.call-update) | async-done | bytes 1048592 | tf_op jit(solution)/shard_map/all_gather | solution.py:190
  36.2 1.3 broadcast_multiply_fusion
  37.5 4.9 %reshape.86 = f32[8,32,4,4,2,32]{5,4,3,2,1,0:T(2,128)} reshape(f32[8,32,1024]{2,1,0:T(8,128)S(1)} %broadcast_multiply_fusion) | data formatting | bytes 2097152 | tf_op jit(solution)/shard_map/reshape | solution.py:191
  42.4 5.6 %copy.33 = f32[8,32,4,4,2,32]{5,2,1,3,4,0:T(4,128)} copy(f32[8,32,4,4,2,32]{5,4,3,2,1,0:T(2,128)} %reshape.86) | data formatting | bytes 2097152 | tf_op jit(solution)/shard_map/reshape | solution.py:191
  48.0 0.0 copy-start.5
  48.0 3.9 %reshape.87.refs_2_ = f32[8,256,128]{2,1,0:T(8,128)S(1)} reshape(f32[8,2,4,32,4,32]{5,4,3,2,1,0:T(4,128)} %bitcast.33) | data formatting | bytes 2097152 | tf_op jit(solution)/shard_map/reshape | solution.py:192
  51.9 32.1 %all-gather.7.cloned.1.call-done = bf16[256,2,32,128]{3,2,1,0:T(8,128)(2,1)} async-done(((bf16[32,2,32,128]{3,2,1,0:T(8,128)(2,1)}), bf16[256,2,32,128]{3,2,1,0:T(8,128)(2,1)}) %all-gather.7.cloned.1.call-update) | async-done | bytes 4194320 | tf_op jit(solution)/shard_map/all_gather | solution.py:188
  84.1 0.0 copy-start.6
  84.1 40.2 %pairs.1 = (f32[8,2,2,32,128]{4,3,2,1,0:T(8,128)}, f32[2,8,2,128]{3,2,1,0:T(2,128)S(1)}) custom-call(s32[10]{0:T(128)S(1)} %pad_add_fusion.refs_0_, bf16[8,32,2,32,128]{4,3,2,1,0:T(8,128)(2,1)} %bitcast.34, f32[8,256,128]{2,1,0:T(8,128)S(1)} %reshape.87.refs_2_, bf16[2,256,768]{2,1,0:T(8,128)(2,1)S(1)} %copy-done.1, bf16[2,256,768]{2,1,0:T(8,128)(2,1)S(1)} %copy-done.2, ...), custom_call_target="tpu_custom_call" | custom-call | tf_op jit(solution)/shard_map/pairs/pallas_call | solution.py:211
  124.2 3.5 %all-to-all-start = ((f32[8,2,2,32,128]{4,3,2,1,0:T(8,128)}), f32[8,2,2,32,128]{4,3,2,1,0:T(8,128)S(1)}, u32[]{:S(2)}, u32[]{:S(2)}) async-start(f32[8,2,2,32,128]{4,3,2,1,0:T(8,128)} %get-tuple-element.5), calls=%async_computation | async-start | bytes 1048576 | tf_op jit(solution)/shard_map/all_to_all | solution.py:223
  127.8 0.1 reduce_sum.24
  127.9 0.1 copy.24
  128.0 44.4 %all-gather.1 = f32[64,8,2]{1,2,0:T(2,128)S(1)} all-gather(f32[2,8,2]{1,2,0:T(2,128)S(1)} %copy.24), channel_id=3, replica_groups=mesh['ka'=4,'ga'=8] {'ka','ga'}, dimensions={0}, use_global_device_ids=true | all-gather | bytes 4224 | tf_op jit(solution)/shard_map/all_gather | solution.py:229
  172.4 0.1 copy.26
  172.5 0.7 copy.27
  173.2 0.6 gather_fusion.2
  173.8 0.6 fusion
  175.0 0.0 all-to-all-done
  175.0 0.8 copy.35
  (19 shorter events, 0.1 us)
Async XLA Ops:
  7.2 13.3 %copy-start = (s32[8,8]{1,0:T(8,128)S(1)}, s32[8,8]{1,0:T(8,128)}, u32[]{:S(2)}) copy-start(s32[8,8]{1,0:T(8,128)} %param.11) | copy-start | bytes 772
  7.2 29.0 %all-gather.5.cloned.1.call-start = ((), (), s32[]{:S(2)}) async-start(), calls=%async_computation.1 | async-start | bytes 1179648 | tf_op jit(solution)/shard_map/all_gather | solution.py:190
  7.9 76.1 %all-gather.7.cloned.1.call-start = ((), (), s32[]{:S(2)}) async-start(), calls=%async_computation.2 | async-start | bytes 4718592 | tf_op jit(solution)/shard_map/all_gather | solution.py:188
  8.0 10.5 %collective-permute-start = (bf16[16,2,32,128]{3,2,1,0:T(8,128)(2,1)}, bf16[16,2,32,128]{3,2,1,0:T(8,128)(2,1)S(1)}, u32[]{:S(2)}, u32[]{:S(2)}) collective-permute-start(bf16[16,2,32,128]{3,2,1,0:T(8,128)(2,1)} %bitcast.38), channel_id=1, source_target_pairs={{0,8},{8,16},{16,24},{24,0},{1,9},{9,17},{17,25},{25,1},{2,10},{10... | collective-permute-start | bytes 786440 | tf_op jit(solution)/shard_map/ppermute | solution.py:187
  48.0 36.1 %copy-start.1 = (bf16[2,256,768]{2,1,0:T(8,128)(2,1)S(1)}, bf16[2,256,768]{2,1,0:T(8,128)(2,1)}, u32[]{:S(2)}) copy-start(bf16[2,256,768]{2,1,0:T(8,128)(2,1)} %constant.104.clone.refs_3_) | copy-start | bytes 2359300
  48.0 36.1 %copy-start.2 = (bf16[2,256,768]{2,1,0:T(8,128)(2,1)S(1)}, bf16[2,256,768]{2,1,0:T(8,128)(2,1)}, u32[]{:S(2)}) copy-start(bf16[2,256,768]{2,1,0:T(8,128)(2,1)} %constant.105.clone.refs_4_) | copy-start | bytes 2359300
  48.0 36.1 %copy-start.3 = (bf16[768,256]{1,0:T(8,128)(2,1)S(1)}, bf16[768,256]{1,0:T(8,128)(2,1)}, u32[]{:S(2)}) copy-start(bf16[768,256]{1,0:T(8,128)(2,1)} %constant.106.clone.refs_5_) | copy-start | bytes 1179652
  48.0 36.1 %copy-start.4 = (bf16[768,256]{1,0:T(8,128)(2,1)S(1)}, bf16[768,256]{1,0:T(8,128)(2,1)}, u32[]{:S(2)}) copy-start(bf16[768,256]{1,0:T(8,128)(2,1)} %constant.107.clone.refs_6_) | copy-start | bytes 1179652
  48.0 36.1 %copy-start.5 = (f32[2,8,128]{2,1,0:T(8,128)S(1)}, f32[2,8,128]{2,1,0:T(8,128)}, u32[]{:S(2)}) copy-start(f32[2,8,128]{2,1,0:T(8,128)} %constant.108.clone.refs_7_) | copy-start | bytes 24580
  84.1 89.7 %copy-start.6 = (s32[8]{0:T(128)S(1)}, s32[8]{0:T(128)}, u32[]{:S(2)}) copy-start(s32[8]{0:T(128)} %param.10) | copy-start | bytes 100
  124.2 50.8 %all-to-all-start = ((f32[8,2,2,32,128]{4,3,2,1,0:T(8,128)}), f32[8,2,2,32,128]{4,3,2,1,0:T(8,128)S(1)}, u32[]{:S(2)}, u32[]{:S(2)}) async-start(f32[8,2,2,32,128]{4,3,2,1,0:T(8,128)} %get-tuple-element.5), calls=%async_computation | async-start | bytes 1048576 | tf_op jit(solution)/shard_map/all_to_all | solution.py:223
Sparse Core Ops, SparseCore 0:
  9.6 26.5 all-gather.4
  38.4 45.6 all-gather.6

commit v2 on v1

--- a/solution.py
+++ b/solution.py
@@ -57,15 +57,21 @@
     return high, low
 
 
-def pair_kernel(rows, bands, windows, points, info, block, kernel, left, left_back, right, right_back,
-                twiddle, out, projections, own, other, total):
+def pair_kernel(rows, bands, windows, points, first, last, info, *refs):
+    mine, refs = refs[0], refs[1:]
+    block, refs = (mine, refs) if first else (refs[0], refs[1:])
+    before, refs = (None, refs) if first else (refs[0], refs[1:])
+    kernel, left, left_back, right, right_back, twiddle, out = refs[:7]
+    projections, refs = (refs[7], refs[8:]) if last else (None, refs[7:])
+    own, other = refs[:2]
+    total = refs[2] if last else out
     members = block.shape[0]
     piece = block.shape[3] // 2
     tall = members * piece
     quads = tall // points
 
-    def load(orbital, part, h):
-        value = block[:, orbital, part, h * piece:(h + 1) * piece, :]
+    def load(orbital, part, h, source=block):
+        value = source[:, orbital, part, h * piece:(h + 1) * piece, :]
         return value.astype(jnp.float32).reshape(tall, LANES)
 
     first_row = info[2 * windows]
@@ -73,8 +79,8 @@
     for r in range(rows):
         for part in range(2):
             for h in range(2):
-                own[r, part, h] = load(first_row + r, part, h)
-    total[...] = jnp.zeros_like(total)
+                own[r, part, h] = load(first_row + r, part, h, mine)
+    total[...] = jnp.zeros_like(total) if first else before[...]
 
     def rotate(real_part, imag_part, p, sign):
         cos = twiddle[0, p * quads:(p + 1) * quads, :].reshape(quads, 1, LANES)
@@ -141,6 +147,8 @@
         return lax.fori_loop(0, info[w], band_body, carry)
 
     lax.fori_loop(0, windows, window_body, 0)
+    if not last:
+        return
     for r in range(rows):
         for part in range(2):
             for h in range(2):
@@ -149,7 +157,7 @@
     def project(a, carry):
         for part in range(2):
             for h in range(2):
-                other[part, h] = load(first_band + a, part, h)
+                other[part, h] = load(first_band + a, part, h, mine)
         for r in range(rows):
             real_sum = jnp.zeros((tall, LANES), jnp.float32)
             imag_sum = jnp.zeros((tall, LANES), jnp.float32)
@@ -176,16 +184,15 @@
     tiles = columns // LANES
     rows = max(1, local * bands // members)
     share = max(1, members // (local * bands))
-    windows = STEPS * local
     tables = build_tables(points, members)
 
     pieces = orbitals.reshape(local * bands, 2, planes, tiles, LANES).transpose(0, 1, 3, 2, 4)
     pieces = pieces.reshape(local * bands, 2, tiles * planes, LANES)
-    blocks = [pieces]
     pairs = [(source, (source + 1) % groups) for source in range(groups)]
+    blocks = [lax.all_gather(pieces, "ga", axis=0)]
     for _ in range(STEPS - 1):
-        blocks.append(lax.ppermute(blocks[-1], "ka", pairs))
-    gathered = lax.all_gather(jnp.concatenate(blocks, axis=0), "ga", axis=0)
+        pieces = lax.ppermute(pieces, "ka", pairs)
+        blocks.append(lax.all_gather(pieces, "ga", axis=0))
 
     whole = lax.all_gather(kernel, "ga", axis=2, tiled=True) * (-1.0 / (kpoints * volume))
     whole = whole.reshape(slots, points, wide, quads, 2, points).transpose(0, 4, 3, 1, 2, 5)
@@ -193,32 +200,45 @@
 
     first_row = member // share * rows
     own_kpoint = first_row // bands
-    anchors = (group - jnp.arange(STEPS, dtype=jnp.int32)) % groups
-    window = (anchors[:, None] * local + jnp.arange(local, dtype=jnp.int32)[None, :]).reshape(-1)
     slot_row = lax.dynamic_index_in_dim(pair_slot, group * local + own_kpoint, 0, keepdims=False)
-    mine = jnp.arange(windows, dtype=jnp.int32) % share == member % share
-    info = jnp.concatenate([jnp.where(mine, band_counts[window], 0), slot_row[window],
-                            jnp.stack([first_row, own_kpoint * bands]).astype(jnp.int32)])
+    mine = jnp.arange(local, dtype=jnp.int32) % share == member % share
+    places = jnp.stack([first_row, own_kpoint * bands]).astype(jnp.int32)
 
     tall = quads * points
     field = (rows, 2, 2, tall, LANES)
     smem = pl.BlockSpec(memory_space=pltpu.SMEM)
     vmem = pl.BlockSpec(memory_space=pltpu.VMEM)
 
-    def body(*refs):
-        pair_kernel(rows, bands, windows, points, *refs)
-
-    spread, projections = pl.pallas_call(
-        body,
-        out_shape=(jax.ShapeDtypeStruct((members, rows, 2, tiles * planes, LANES), jnp.float32),
-                   jax.ShapeDtypeStruct((rows, bands, 2, LANES), jnp.float32)),
-        in_specs=[smem] + [vmem] * 7,
-        out_specs=(vmem, vmem),
-        scratch_shapes=[pltpu.VMEM(field, jnp.float32), pltpu.VMEM(field[1:], jnp.float32),
-                        pltpu.VMEM(field, jnp.float32)],
-        compiler_params=pltpu.CompilerParams(vmem_limit_bytes=48 * 2 ** 20),
-        name="pairs",
-    )(info, gathered, whole, *[jnp.asarray(table) for table in tables])
+    tables = [jnp.asarray(table) for table in tables]
+    state = []
+    for step in range(STEPS):
+        first, last = step == 0, step == STEPS - 1
+        anchor = (group - step) % groups * local
+        counts = lax.dynamic_slice_in_dim(band_counts, anchor, local)
+        chosen = lax.dynamic_slice_in_dim(slot_row, anchor, local)
+        info = jnp.concatenate([jnp.where(mine, counts, 0), chosen, places])
+        operands = blocks[:1] + ([] if first else [blocks[step]] + state) + [whole] + tables
+        results = [jax.ShapeDtypeStruct(field, jnp.float32)]
+        scratch = [pltpu.VMEM(field, jnp.float32), pltpu.VMEM(field[1:], jnp.float32)]
+        if last:
+            results = [jax.ShapeDtypeStruct((members, rows, 2, tiles * planes, LANES), jnp.float32),
+                       jax.ShapeDtypeStruct((rows, bands, 2, LANES), jnp.float32)]
+            scratch.append(pltpu.VMEM(field, jnp.float32))
+
+        def body(*refs, first=first, last=last):
+            pair_kernel(rows, bands, local, points, first, last, *refs)
+
+        state = list(pl.pallas_call(
+            body,
+            out_shape=results,
+            in_specs=[smem] + [vmem] * len(operands),
+            out_specs=[vmem] * len(results),
+            scratch_shapes=scratch,
+            compiler_params=pltpu.CompilerParams(vmem_limit_bytes=32 * 2 ** 20),
+            cost_estimate=pl.CostEstimate(flops=20 * 10 ** 9, bytes_accessed=8 * 2 ** 20, transcendentals=0),
+            name=f"pairs_{step}",
+        )(info, *operands))
+    spread, projections = state
 
     vectors = lax.all_to_all(spread, "ga", split_axis=0, concat_axis=0, tiled=True)
     if share > 1:
@@ -226,9 +246,10 @@
     vectors = vectors.reshape(local, bands, 2, tiles, planes, LANES).transpose(0, 1, 2, 4, 3, 5)
     vectors = vectors.reshape(local, bands, 2, planes, columns)
     sums = jnp.sum(projections, axis=-1) / volume
-    sums = lax.all_gather(sums, ("ka", "ga"), axis=0)
-    sums = jnp.sum(sums.reshape(kpoints, bands, share, bands, 2), axis=2)
-    everything = sums.transpose(0, 3, 2, 1)
+    everything = jnp.zeros((kpoints, 2, bands, bands), jnp.float32)
+    everything = lax.dynamic_update_slice(
+        everything, sums.transpose(2, 1, 0)[None], (group * local + own_kpoint, 0, 0, first_row % bands))
+    everything = lax.psum(everything, ("ka", "ga"))
     matrix = lax.dynamic_slice_in_dim(everything, group * local, local, 0)
     occupied = (jnp.arange(bands)[None, :] < band_counts[:, None]).astype(jnp.float32)
     energy = jnp.sum(occupied * jnp.diagonal(everything[:, 0], axis1=1, axis2=2)) / (2.0 * kpoints)

time: 183 us -> 188 us (1.027); the launches traced: 184 us -> 187 us
  local copies, waits for them, and re-layouts: 18.7 us -> 32.8 us
  waiting for transfers between devices: 54 us -> 43.8 us
  blocking collectives: 44.4 us -> 52.4 us
  Pallas kernels: 40.2 us -> 33.3 us
    psum x0 -> x1, blocking collectives: none -> 52.4 us  [on_device(): everything = lax.psum(everything, ('ka', 'ga'))]
    all_gather x1 -> x0, blocking collectives: 44.4 us -> none  [on_device(): sums = lax.all_gather(sums, ('ka', 'ga'), axis=0)]
    unnamed x16 -> x34, local copies, waits for them, and re-layouts: 1.52 us -> 15.8 us
    all_gather x1 -> x2, waiting for transfers between devices: 32.1 us -> 20.5 us  [the longest x1 14.2 us: on_device(): blocks = [lax.all_gather(pieces, 'ga', axis=0)]]
    pallas_call x1 -> x2, Pallas kernels: 40.2 us -> 33.3 us  [on_device(): pl.pallas_call(body, out_shape=results, in_specs=[smem] + [vmem] * len(op...]
    gather x2 -> x0, local copies, waits for them, and re-layouts: 1.93 us -> none  [the longest x1 1.29 us: on_device(): band_counts[window]]
  transfers between devices with their start and end apart: 4 -> 5, of which waited for: 3 -> 4; matrix products, arithmetic and copies ran while one was open for 12% -> 11% of each run, Pallas kernels for 0% -> 9%
where the time goes in v2:
time: 188 us; the launch traced here: 187 us
  blocking collectives  52.4 us (28%)
  waiting for transfers between devices  43.8 us (23%)
  Pallas kernels  33.3 us (18%)
  local copies, waits for them, and re-layouts  32.8 us (17%)
  between operations  15.7 us (8%)
  starting transfers between devices  6.63 us (4%)
  other arithmetic  2.12 us (1%)
    psum x1, blocking collectives, on_device(): everything = lax.psum(everything, ('ka', 'ga'))  52.4 us
    pallas_call x2, Pallas kernels, on_device(): pl.pallas_call(body, out_shape=results, in_specs=[smem] + [vmem] * len(op...  33.3 us
    unnamed x34, local copies, waits for them, and re-layouts  15.8 us
    all_gather x1, waiting for transfers between devices, on_device(): lax.all_gather(kernel, 'ga', axis=2, tiled=True)  14.5 us
    all_gather x1, waiting for transfers between devices, on_device(): blocks = [lax.all_gather(pieces, 'ga', axis=0)]  14.2 us
    reshape x2, local copies, waits for them, and re-layouts, on_device(): whole.reshape(slots, points, wide, quads, 2, points)  10.4 us
    ppermute x1, waiting for transfers between devices, on_device(): pieces = lax.ppermute(pieces, 'ka', pairs)  7.47 us
    all_gather x1, waiting for transfers between devices, on_device(): blocks.append(lax.all_gather(pieces, 'ga', axis=0))  6.3 us
  transfers between devices with their start and end apart: 5, of which 4 were waited for; matrix products, arithmetic and copies ran while one was open for 11% of the time, Pallas kernels for 9%

profile of v2, /device:TPU:0, one launch (start us, length us, event | category | flops | bytes accessed | tf_op | source)
XLA Modules:
  0.0 186.8 jit_solution(12634721445046173209)
XLA Ops:
  7.2 0.7 all-gather.7.cloned.1.call-update
  7.9 0.7 all-gather.5.cloned.1.call-update
  8.7 3.0 %collective-permute-start = (bf16[16,2,32,128]{3,2,1,0:T(8,128)(2,1)}, bf16[16,2,32,128]{3,2,1,0:T(8,128)(2,1)S(1)}, u32[]{:S(2)}, u32[]{:S(2)}) collective-permute-start(bf16[16,2,32,128]{3,2,1,0:T(8,128)(2,1)} %bitcast.38), channel_id=1, source_target_pairs={{0,8},{8,16},{16,24},{24,0},{1,9},{9,17},{17,25},{25,1},{2,10},{10... | collective-permute-start | bytes 786440 | tf_op jit(solution)/shard_map/ppermute | solution.py:194
  11.7 7.5 %collective-permute-done = bf16[16,2,32,128]{3,2,1,0:T(8,128)(2,1)S(1)} collective-permute-done((bf16[16,2,32,128]{3,2,1,0:T(8,128)(2,1)}, bf16[16,2,32,128]{3,2,1,0:T(8,128)(2,1)S(1)}, u32[]{:S(2)}, u32[]{:S(2)}) %collective-permute-start) | collective-permute-done | bytes 262176 | tf_op jit(solution)/shard_map/ppermute | solution.py:194
  19.2 0.7 copy-done.14
  20.0 0.8 fusion.1
  20.8 0.8 dynamic-slice_bitcast_fusion
  21.7 14.5 %all-gather.7.cloned.1.call-done = f32[8,32,1024]{2,1,0:T(8,128)} async-done(((f32[8,32,128]{2,1,0:T(8,128)}), f32[8,32,1024]{2,1,0:T(8,128)}) %all-gather.7.cloned.1.call-update) | async-done | bytes 1048592 | tf_op jit(solution)/shard_map/all_gather | solution.py:197
  36.2 1.3 broadcast_multiply_fusion
  37.5 4.9 %reshape.29 = f32[8,32,4,4,2,32]{5,4,3,2,1,0:T(2,128)} reshape(f32[8,32,1024]{2,1,0:T(8,128)S(1)} %broadcast_multiply_fusion) | data formatting | bytes 2097152 | tf_op jit(solution)/shard_map/reshape | solution.py:198
  42.4 5.5 %copy.26 = f32[8,32,4,4,2,32]{5,2,1,3,4,0:T(4,128)} copy(f32[8,32,4,4,2,32]{5,4,3,2,1,0:T(2,128)} %reshape.29) | data formatting | bytes 2097152 | tf_op jit(solution)/shard_map/reshape | solution.py:198
  47.9 3.8 %reshape.30.refs_2_.refs_4_ = f32[8,256,128]{2,1,0:T(8,128)S(1)} reshape(f32[8,2,4,32,4,32]{5,4,3,2,1,0:T(4,128)} %bitcast.35) | data formatting | bytes 2097152 | tf_op jit(solution)/shard_map/reshape | solution.py:199
  51.7 14.2 %all-gather.5.cloned.1.call-done.refs_1_ = bf16[8,16,2,32,128]{4,3,2,1,0:T(8,128)(2,1)} async-done(((bf16[1,16,2,32,128]{4,3,2,1,0:T(8,128)(2,1)}), bf16[8,16,2,32,128]{4,3,2,1,0:T(8,128)(2,1)}) %all-gather.5.cloned.1.call-update) | async-done | bytes 2097168 | tf_op jit(solution)/shard_map/all_gather | solution.py:192
  65.9 1.6 copy-done
  67.5 1.1 copy-done.3
  68.6 1.1 copy-done.5
  69.7 1.0 copy-done.7
  70.7 1.0 copy-done.9
  71.7 17.2 %pairs_0.1.refs_3_ = f32[2,2,2,128,128]{4,3,2,1,0:T(8,128)S(1)} custom-call(s32[6]{0:T(128)S(1)} %get-tuple-element.18.refs_0_, bf16[8,16,2,32,128]{4,3,2,1,0:T(8,128)(2,1)S(1)} %copy-done, f32[8,256,128]{2,1,0:T(8,128)S(1)} %reshape.30.refs_2_.refs_4_, bf16[2,256,768]{2,1,0:T(8,128)(2,1)S(1)} %copy-done.3, bf16[2,256,768]{2,1,0:T(8,128)(2,1)S(1)} %copy-done.5, ...), custom_call_target="tpu_custom_call" | custom-call | flops 20000000000 | bytes 8388608 | tf_op jit(solution)/shard_map/pairs_0/pallas_call | solution.py:231
  89.0 0.8 copy-done.12
  89.7 6.3 %all-gather.9.cloned.1.call-done = bf16[128,2,32,128]{3,2,1,0:T(8,128)(2,1)} async-done(((bf16[16,2,32,128]{3,2,1,0:T(8,128)(2,1)}), bf16[128,2,32,128]{3,2,1,0:T(8,128)(2,1)}) %all-gather.9.cloned.1.call-update) | async-done | bytes 2097168 | tf_op jit(solution)/shard_map/all_gather | solution.py:195
  96.0 1.6 copy-done.2
  97.6 1.1 copy-done.4
  98.8 1.1 copy-done.6
  99.9 1.0 copy-done.8
  100.9 1.0 copy-done.10
  101.9 1.0 copy-done.13
  102.9 16.1 %pairs_1.1 = (f32[8,2,2,32,128]{4,3,2,1,0:T(8,128)}, f32[2,8,2,128]{3,2,1,0:T(2,128)S(1)}) custom-call(s32[6]{0:T(128)S(1)} %get-tuple-element.17.refs_0_, bf16[8,16,2,32,128]{4,3,2,1,0:T(8,128)(2,1)S(1)} %copy-done.1, bf16[8,16,2,32,128]{4,3,2,1,0:T(8,128)(2,1)S(1)} %bitcast.34, f32[2,2,2,128,128]{4,3,2,1,0:T(8,128)S(1)} %copy-done.13, ...), custom_call_target="tpu_custom_call" | custom-call | flops 20000000000 | bytes 8388608 | tf_op jit(solution)/shard_map/pairs_1/pallas_call | solution.py:231
  119.0 3.5 %all-to-all-start = ((f32[8,2,2,32,128]{4,3,2,1,0:T(8,128)}), f32[8,2,2,32,128]{4,3,2,1,0:T(8,128)S(1)}, u32[]{:S(2)}, u32[]{:S(2)}) async-start(f32[8,2,2,32,128]{4,3,2,1,0:T(8,128)} %get-tuple-element.5), calls=%async_computation | async-start | bytes 1048576 | tf_op jit(solution)/shard_map/all_to_all | solution.py:243
  123.2 52.4 %psum.7 = f32[8,2,8,8]{0,3,2,1:T(8,128)S(1)} all-reduce(f32[8,2,8,8]{0,3,2,1:T(8,128)S(1)} %dynamic_update_slice.3), channel_id=1, replica_groups=mesh['ka'=4,'ga'=8] {'ka','ga'}, use_global_device_ids=true, to_apply=%region_1.2 | all-reduce | flops 1024 | bytes 8192 | tf_op jit(solution)/shard_map/psum | solution.py:252
  175.7 0.8 copy.22
  178.3 0.8 copy.29
  (35 shorter events, 2.2 us)
Async XLA Ops:
  7.2 29.0 %all-gather.7.cloned.1.call-start = ((), (), s32[]{:S(2)}) async-start(), calls=%async_computation.2 | async-start | bytes 1179648 | tf_op jit(solution)/shard_map/all_gather | solution.py:197
  7.9 58.0 %all-gather.5.cloned.1.call-start = ((), (), s32[]{:S(2)}) async-start(), calls=%async_computation.1 | async-start | bytes 2359296 | tf_op jit(solution)/shard_map/all_gather | solution.py:192
  8.6 87.4 %all-gather.9.cloned.1.call-start = ((), (), s32[]{:S(2)}) async-start(), calls=%async_computation.3 | async-start | bytes 2359296 | tf_op jit(solution)/shard_map/all_gather | solution.py:195
  8.7 10.5 %collective-permute-start = (bf16[16,2,32,128]{3,2,1,0:T(8,128)(2,1)}, bf16[16,2,32,128]{3,2,1,0:T(8,128)(2,1)S(1)}, u32[]{:S(2)}, u32[]{:S(2)}) collective-permute-start(bf16[16,2,32,128]{3,2,1,0:T(8,128)(2,1)} %bitcast.38), channel_id=1, source_target_pairs={{0,8},{8,16},{16,24},{24,0},{1,9},{9,17},{17,25},{25,1},{2,10},{10... | collective-permute-start | bytes 786440 | tf_op jit(solution)/shard_map/ppermute | solution.py:194
  19.2 0.7 copy-start.14
  47.9 17.9 %copy-start.11 = (f32[2,8,128]{2,1,0:T(8,128)S(1)}, f32[2,8,128]{2,1,0:T(8,128)}, u32[]{:S(2)}) copy-start(f32[2,8,128]{2,1,0:T(8,128)} %constant.137.clone.refs_7_.refs_9_) | copy-start | bytes 24580
  65.9 1.6 copy-start
  67.4 1.1 copy-start.3
  68.6 1.1 copy-start.5
  69.7 1.0 copy-start.7
  70.7 1.0 copy-start.9
  71.7 24.3 %copy-start.1 = (bf16[8,16,2,32,128]{4,3,2,1,0:T(8,128)(2,1)S(1)}, bf16[8,16,2,32,128]{4,3,2,1,0:T(8,128)(2,1)}, u32[]{:S(2)}) copy-start(bf16[8,16,2,32,128]{4,3,2,1,0:T(8,128)(2,1)} %all-gather.5.cloned.1.call-done.refs_1_) | copy-start | bytes 6291460
  88.9 0.8 copy-start.12
  96.0 1.6 copy-start.2
  97.6 1.1 copy-start.4
  98.8 1.1 copy-start.6
  99.9 1.0 copy-start.8
  100.9 1.0 copy-start.10
  101.9 1.0 copy-start.13
  102.9 74.1 %copy-start.15 = (s32[8]{0:T(128)S(1)}, s32[8]{0:T(128)}, u32[]{:S(2)}) copy-start(s32[8]{0:T(128)} %param.10) | copy-start | bytes 100
  119.0 59.3 %all-to-all-start = ((f32[8,2,2,32,128]{4,3,2,1,0:T(8,128)}), f32[8,2,2,32,128]{4,3,2,1,0:T(8,128)S(1)}, u32[]{:S(2)}, u32[]{:S(2)}) async-start(f32[8,2,2,32,128]{4,3,2,1,0:T(8,128)} %get-tuple-element.5), calls=%async_computation | async-start | bytes 1048576 | tf_op jit(solution)/shard_map/all_to_all | solution.py:243
Sparse Core Ops, SparseCore 0:
  9.6 26.5 all-gather.6
  37.8 28.0 all-gather.4
  67.5 28.5 all-gather.8

commit v3 on v1

--- a/solution.py
+++ b/solution.py
@@ -220,18 +220,27 @@
         name="pairs",
     )(info, gathered, whole, *[jnp.asarray(table) for table in tables])
 
-    vectors = lax.all_to_all(spread, "ga", split_axis=0, concat_axis=0, tiled=True)
+    copies = jnp.broadcast_to(projections.transpose(0, 2, 1, 3)[None], (members, rows, 2, bands, LANES))
+    arrived = lax.all_to_all(jnp.concatenate([spread, copies], axis=3), "ga", split_axis=0, concat_axis=0, tiled=True)
+    arrived = arrived.reshape(members * rows, 2, tiles * planes + bands, LANES)
+    vectors = arrived[:, :, :tiles * planes]
+    projections = arrived[:, :, tiles * planes:].reshape(local * bands, share, 2, bands, LANES).transpose(0, 1, 3, 2, 4)
     if share > 1:
         vectors = jnp.sum(vectors.reshape(local * bands, share, *vectors.shape[1:]), axis=1)
     vectors = vectors.reshape(local, bands, 2, tiles, planes, LANES).transpose(0, 1, 2, 4, 3, 5)
     vectors = vectors.reshape(local, bands, 2, planes, columns)
-    sums = jnp.sum(projections, axis=-1) / volume
-    sums = lax.all_gather(sums, ("ka", "ga"), axis=0)
-    sums = jnp.sum(sums.reshape(kpoints, bands, share, bands, 2), axis=2)
-    everything = sums.transpose(0, 3, 2, 1)
-    matrix = lax.dynamic_slice_in_dim(everything, group * local, local, 0)
-    occupied = (jnp.arange(bands)[None, :] < band_counts[:, None]).astype(jnp.float32)
-    energy = jnp.sum(occupied * jnp.diagonal(everything[:, 0], axis1=1, axis2=2)) / (2.0 * kpoints)
+    sums = jnp.sum(jnp.sum(projections, axis=-1) / volume, axis=1)
+    matrix = sums.reshape(local, bands, bands, 2).transpose(0, 3, 2, 1)
+    own_counts = lax.dynamic_slice_in_dim(band_counts, group * local, local)
+    occupied = (jnp.arange(bands)[None, :] < own_counts[:, None]).astype(jnp.float32)
+    part = jnp.sum(occupied * jnp.diagonal(matrix[:, 0], axis1=1, axis2=2)) / (2.0 * kpoints)
+    place = jnp.arange(groups, dtype=jnp.int32)
+    terms = jnp.where(place == group, part, 0.0)
+    for step in range(1, groups):
+        ring = [(source, (source + step) % groups) for source in range(groups)]
+        arrived = lax.ppermute(part.reshape(1), "ka", ring)
+        terms = jnp.where(place == (group - step) % groups, arrived, terms)
+    energy = jnp.sum(terms)
     return (vectors, matrix, energy)
 
 

time: 183 us -> 170 us (0.929)
  blocking collectives: 44.4 us -> 0 us
  starting transfers between devices: 6.59 us -> 27.6 us
  waiting for transfers between devices: 54 us -> 73.5 us
  Pallas kernels: 40.2 us -> 30.1 us
  other arithmetic: 3.97 us -> 7.33 us
    all_gather x1 -> x0, blocking collectives: 44.4 us -> none  [on_device(): sums = lax.all_gather(sums, ('ka', 'ga'), axis=0)]
    ppermute x0 -> x3, starting transfers between devices: none -> 21 us  [on_device(): arrived = lax.ppermute(part.reshape(1), 'ka', ring)]
    all_to_all x1, waiting for transfers between devices: 0.01 us -> 17.9 us  [on_device(): lax.all_to_all(jnp.concatenate([spread, copies], axis=3), 'ga', split_axi...]
    pallas_call x1, Pallas kernels: 40.2 us -> 30.1 us  [on_device(): pl.pallas_call(body, out_shape=(jax.ShapeDtypeStruct((members, rows, 2, t...]
    reduce_sum x2 -> x3, other arithmetic: 0.69 us -> 3.14 us  [the longest x1 2.42 us: on_device(): energy = jnp.sum(terms)]
  transfers between devices with their start and end apart: 4 -> 7, of which waited for: 3 -> 5; matrix products, arithmetic and copies ran while one was open for 12% -> 12% of each run, Pallas kernels for 0% -> 0%
where the time goes in v3:
time: 170 us; the launch traced here: 172 us
  waiting for transfers between devices  73.5 us (43%)
  Pallas kernels  30.1 us (18%)
  starting transfers between devices  27.6 us (16%)
  local copies, waits for them, and re-layouts  19 us (11%)
  between operations  14.9 us (9%)
  other arithmetic  7.33 us (4%)
    all_gather x1, waiting for transfers between devices, on_device(): gathered = lax.all_gather(jnp.concatenate(blocks, axis=0), 'ga', axis=0)  32.1 us
    pallas_call x1, Pallas kernels, on_device(): pl.pallas_call(body, out_shape=(jax.ShapeDtypeStruct((members, rows, 2, t...  30.1 us
    ppermute x3, starting transfers between devices, on_device(): arrived = lax.ppermute(part.reshape(1), 'ka', ring)  21 us
    all_to_all x1, waiting for transfers between devices, on_device(): lax.all_to_all(jnp.concatenate([spread, copies], axis=3), 'ga', split_axi...  17.9 us
    all_gather x1, waiting for transfers between devices, on_device(): lax.all_gather(kernel, 'ga', axis=2, tiled=True)  13.7 us
    reshape x2, local copies, waits for them, and re-layouts, on_device(): whole.reshape(slots, points, wide, quads, 2, points)  10.5 us
    ppermute x1, waiting for transfers between devices, on_device(): blocks.append(lax.ppermute(blocks[-1], 'ka', pairs))  7.47 us
    reshape x1, local copies, waits for them, and re-layouts, on_device(): whole = whole.reshape(slots, 2 * quads * points, LANES)  3.9 us
  transfers between devices with their start and end apart: 7, of which 5 were waited for; matrix products, arithmetic and copies ran while one was open for 12% of the time, Pallas kernels for 0%

profile of v3, /device:TPU:0, one launch (start us, length us, event | category | flops | bytes accessed | tf_op | source)
XLA Modules:
  0.0 172.4 jit_solution(10427693084097187502)
XLA Ops:
  7.2 0.7 all-gather.4.cloned.1.call-update
  8.0 3.0 %collective-permute-start = (bf16[16,2,32,128]{3,2,1,0:T(8,128)(2,1)}, bf16[16,2,32,128]{3,2,1,0:T(8,128)(2,1)S(1)}, u32[]{:S(2)}, u32[]{:S(2)}) collective-permute-start(bf16[16,2,32,128]{3,2,1,0:T(8,128)(2,1)} %bitcast.50), channel_id=1, source_target_pairs={{0,8},{8,16},{16,24},{24,0},{1,9},{9,17},{17,25},{25,1},{2,10},{10... | collective-permute-start | bytes 786440 | tf_op jit(solution)/shard_map/ppermute | solution.py:187
  11.0 7.5 %collective-permute-done = bf16[16,2,32,128]{3,2,1,0:T(8,128)(2,1)S(1)} collective-permute-done((bf16[16,2,32,128]{3,2,1,0:T(8,128)(2,1)}, bf16[16,2,32,128]{3,2,1,0:T(8,128)(2,1)S(1)}, u32[]{:S(2)}, u32[]{:S(2)}) %collective-permute-start) | collective-permute-done | bytes 262176 | tf_op jit(solution)/shard_map/ppermute | solution.py:187
  18.5 1.8 %pad_maximum_fusion.1 = bf16[32,2,32,128]{3,2,1,0:T(8,128)(2,1)} fusion(bf16[16,2,32,128]{3,2,1,0:T(8,128)(2,1)S(1)} %collective-permute-done, bf16[16,2,32,128]{3,2,1,0:T(8,128)(2,1)} %bitcast.51), kind=kLoop, calls=%fused_computation.5 | loop fusion | flops 262144 | bytes 1048576 | tf_op jit(solution)/shard_map/concatenate | solution.py:188
  20.3 0.1 iota_add_fusion
  20.4 0.1 add.83
  20.5 0.6 gather_fusion.1
  21.1 1.3 gather_fusion
  22.4 0.1 pad_add_fusion.refs_0_
  22.5 13.7 %all-gather.4.cloned.1.call-done = f32[8,32,1024]{2,1,0:T(8,128)} async-done(((f32[8,32,128]{2,1,0:T(8,128)}), f32[8,32,1024]{2,1,0:T(8,128)}) %all-gather.4.cloned.1.call-update) | async-done | bytes 1048592 | tf_op jit(solution)/shard_map/all_gather | solution.py:190
  36.2 1.3 broadcast_multiply_fusion
  37.5 4.9 %reshape.92 = f32[8,32,4,4,2,32]{5,4,3,2,1,0:T(2,128)} reshape(f32[8,32,1024]{2,1,0:T(8,128)S(1)} %broadcast_multiply_fusion) | data formatting | bytes 2097152 | tf_op jit(solution)/shard_map/reshape | solution.py:191
  42.4 5.6 %copy.39 = f32[8,32,4,4,2,32]{5,2,1,3,4,0:T(4,128)} copy(f32[8,32,4,4,2,32]{5,4,3,2,1,0:T(2,128)} %reshape.92) | data formatting | bytes 2097152 | tf_op jit(solution)/shard_map/reshape | solution.py:191
  48.0 3.9 %reshape.93.refs_2_ = f32[8,256,128]{2,1,0:T(8,128)S(1)} reshape(f32[8,2,4,32,4,32]{5,4,3,2,1,0:T(4,128)} %bitcast.44) | data formatting | bytes 2097152 | tf_op jit(solution)/shard_map/reshape | solution.py:192
  51.9 32.1 %all-gather.6.cloned.1.call-done = bf16[256,2,32,128]{3,2,1,0:T(8,128)(2,1)} async-done(((bf16[32,2,32,128]{3,2,1,0:T(8,128)(2,1)}), bf16[256,2,32,128]{3,2,1,0:T(8,128)(2,1)}) %all-gather.6.cloned.1.call-update) | async-done | bytes 4194320 | tf_op jit(solution)/shard_map/all_gather | solution.py:188
  84.1 30.1 %pairs.1 = (f32[8,2,2,32,128]{4,3,2,1,0:T(8,128)S(1)}, f32[2,8,2,128]{3,2,1,0:T(2,128)S(1)}) custom-call(s32[10]{0:T(128)S(1)} %pad_add_fusion.refs_0_, bf16[8,32,2,32,128]{4,3,2,1,0:T(8,128)(2,1)} %bitcast.45, f32[8,256,128]{2,1,0:T(8,128)S(1)} %reshape.93.refs_2_, bf16[2,256,768]{2,1,0:T(8,128)(2,1)S(1)} %copy-done.1, bf16[2,256,768]{2,1,0:T(8,128)(2,1)S(1)} %copy-done.2, ...), custom_call_target="tpu_custom_call" | custom-call | tf_op jit(solution)/shard_map/pairs/pallas_call | solution.py:211
  114.2 0.9 pad_maximum_fusion
  115.1 3.5 %all-to-all-start = ((f32[8,2,2,40,128]{4,3,2,1,0:T(8,128)}), f32[8,2,2,40,128]{4,3,2,1,0:T(8,128)S(1)}, u32[]{:S(2)}, u32[]{:S(2)}) async-start(f32[8,2,2,40,128]{4,3,2,1,0:T(8,128)} %pad_maximum_fusion), calls=%async_computation | async-start | bytes 1310720 | tf_op jit(solution)/shard_map/all_to_all | solution.py:224
  118.7 0.1 dynamic_slice.8
  118.8 17.9 %all-to-all-done = f32[8,2,2,40,128]{4,3,2,1,0:T(8,128)S(1)} async-done(((f32[8,2,2,40,128]{4,3,2,1,0:T(8,128)}), f32[8,2,2,40,128]{4,3,2,1,0:T(8,128)S(1)}, u32[]{:S(2)}, u32[]{:S(2)}) %all-to-all-start) | async-done | bytes 655392 | tf_op jit(solution)/shard_map/all_to_all | solution.py:224
  136.7 0.1 slice_reduce_fusion
  136.9 0.1 copy.33
  137.0 0.1 copy.31
  137.1 0.6 gather_fusion.2
  137.7 0.6 fusion
  138.9 1.4 collective-permute-start.1
  140.3 18.3 %collective-permute-start.2 = (f32[1]{0:T(128)}, f32[1]{0:T(128)}, u32[]{:S(2)}, u32[]{:S(2)}) collective-permute-start(f32[1]{0:T(128)} %bitcast.25), channel_id=1, source_target_pairs={{0,16},{8,24},{16,0},{24,8},{1,17},{9,25},{17,1},{25,9},{2,18},{10... | collective-permute-start | bytes 20 | tf_op jit(solution)/shard_map/ppermute | solution.py:241
  158.6 1.3 collective-permute-start.3
  160.0 1.0 reshape.96
  161.0 0.7 copy.32
  161.6 1.5 collective-permute-done.3
  163.2 2.4 %fusion.2 = f32[]{:T(128)} fusion(f32[]{:T(128)} %div.29, s32[]{:T(128)S(6)} %axis_index.23, f32[]{:T(128)} %bitcast.28, s32[]{:T(128)S(6)} %select_n.82, f32[]{:T(128)} %bitcast.27, s32[]{:T(128)S(6)} %select_n.81, f32[]{:T(128)} %bitcast.26, s32[]{:T(128)S(6)} %select_n.79), kind=kLoop, calls=%fused_computation.25 | loop fusion | flops 35 | bytes 36 | tf_op jit(solution)/shard_map/reduce_sum | solution.py:243
  (30 shorter events, 0.3 us)
Async XLA Ops:
  7.2 13.3 %copy-start = (s32[8,8]{1,0:T(8,128)S(1)}, s32[8,8]{1,0:T(8,128)}, u32[]{:S(2)}) copy-start(s32[8,8]{1,0:T(8,128)} %param.11) | copy-start | bytes 772
  7.2 29.0 %all-gather.4.cloned.1.call-start = ((), (), s32[]{:S(2)}) async-start(), calls=%async_computation.1 | async-start | bytes 1179648 | tf_op jit(solution)/shard_map/all_gather | solution.py:190
  7.9 76.1 %all-gather.6.cloned.1.call-start = ((), (), s32[]{:S(2)}) async-start(), calls=%async_computation.2 | async-start | bytes 4718592 | tf_op jit(solution)/shard_map/all_gather | solution.py:188
  8.0 10.5 %collective-permute-start = (bf16[16,2,32,128]{3,2,1,0:T(8,128)(2,1)}, bf16[16,2,32,128]{3,2,1,0:T(8,128)(2,1)S(1)}, u32[]{:S(2)}, u32[]{:S(2)}) collective-permute-start(bf16[16,2,32,128]{3,2,1,0:T(8,128)(2,1)} %bitcast.50), channel_id=1, source_target_pairs={{0,8},{8,16},{16,24},{24,0},{1,9},{9,17},{17,25},{25,1},{2,10},{10... | collective-permute-start | bytes 786440 | tf_op jit(solution)/shard_map/ppermute | solution.py:187
  48.0 36.1 %copy-start.1 = (bf16[2,256,768]{2,1,0:T(8,128)(2,1)S(1)}, bf16[2,256,768]{2,1,0:T(8,128)(2,1)}, u32[]{:S(2)}) copy-start(bf16[2,256,768]{2,1,0:T(8,128)(2,1)} %constant.122.clone.refs_3_) | copy-start | bytes 2359300
  48.0 36.1 %copy-start.2 = (bf16[2,256,768]{2,1,0:T(8,128)(2,1)S(1)}, bf16[2,256,768]{2,1,0:T(8,128)(2,1)}, u32[]{:S(2)}) copy-start(bf16[2,256,768]{2,1,0:T(8,128)(2,1)} %constant.123.clone.refs_4_) | copy-start | bytes 2359300
  48.0 36.1 %copy-start.3 = (bf16[768,256]{1,0:T(8,128)(2,1)S(1)}, bf16[768,256]{1,0:T(8,128)(2,1)}, u32[]{:S(2)}) copy-start(bf16[768,256]{1,0:T(8,128)(2,1)} %constant.124.clone.refs_5_) | copy-start | bytes 1179652
  48.0 36.1 %copy-start.4 = (bf16[768,256]{1,0:T(8,128)(2,1)S(1)}, bf16[768,256]{1,0:T(8,128)(2,1)}, u32[]{:S(2)}) copy-start(bf16[768,256]{1,0:T(8,128)(2,1)} %constant.125.clone.refs_6_) | copy-start | bytes 1179652
  48.0 36.1 %copy-start.5 = (f32[2,8,128]{2,1,0:T(8,128)S(1)}, f32[2,8,128]{2,1,0:T(8,128)}, u32[]{:S(2)}) copy-start(f32[2,8,128]{2,1,0:T(8,128)} %constant.126.clone.refs_7_) | copy-start | bytes 24580
  84.1 34.6 %copy-start.6 = (s32[8]{0:T(128)S(1)}, s32[8]{0:T(128)}, u32[]{:S(2)}) copy-start(s32[8]{0:T(128)} %param.10) | copy-start | bytes 100
  115.1 21.6 %all-to-all-start = ((f32[8,2,2,40,128]{4,3,2,1,0:T(8,128)}), f32[8,2,2,40,128]{4,3,2,1,0:T(8,128)S(1)}, u32[]{:S(2)}, u32[]{:S(2)}) async-start(f32[8,2,2,40,128]{4,3,2,1,0:T(8,128)} %pad_maximum_fusion), calls=%async_computation | async-start | bytes 1310720 | tf_op jit(solution)/shard_map/all_to_all | solution.py:224
  138.9 22.7 %collective-permute-start.1 = (f32[1]{0:T(128)}, f32[1]{0:T(128)}, u32[]{:S(2)}, u32[]{:S(2)}) collective-permute-start(f32[1]{0:T(128)} %bitcast.25), channel_id=1, source_target_pairs={{0,24},{8,0},{16,8},{24,16},{1,25},{9,1},{17,9},{25,17},{2,26},{10... | collective-permute-start | bytes 20 | tf_op jit(solution)/shard_map/ppermute | solution.py:241
  140.3 21.4 %collective-permute-start.2 = (f32[1]{0:T(128)}, f32[1]{0:T(128)}, u32[]{:S(2)}, u32[]{:S(2)}) collective-permute-start(f32[1]{0:T(128)} %bitcast.25), channel_id=1, source_target_pairs={{0,16},{8,24},{16,0},{24,8},{1,17},{9,25},{17,1},{25,9},{2,18},{10... | collective-permute-start | bytes 20 | tf_op jit(solution)/shard_map/ppermute | solution.py:241
  158.6 4.6 %collective-permute-start.3 = (f32[1]{0:T(128)}, f32[1]{0:T(128)}, u32[]{:S(2)}, u32[]{:S(2)}) collective-permute-start(f32[1]{0:T(128)} %bitcast.25), channel_id=1, source_target_pairs={{0,8},{8,16},{16,24},{24,0},{1,9},{9,17},{17,25},{25,1},{2,10},{10... | collective-permute-start | bytes 20 | tf_op jit(solution)/shard_map/ppermute | solution.py:241
Sparse Core Ops, SparseCore 0:
  9.6 26.5 all-gather.3
  38.4 45.6 all-gather.5
